TPU v7x, 32 devices: a whole 2x2x4 slice. The times are simulated.
32 devices in a mesh: row: 4 (over x, core), col: 8 (over z, y).
Axes of the slice: x: 2, y: 2, z: 4, core: 2. Of those that a mesh axis runs over, the one named last changes fastest.
Arguments:
- tiles: int32 [4, 8, 8, 128, 128], P('row', 'col'), may hold values from 0 to 1073741823, as said below
- slots: int32 [4, 8, 8], P('row', 'col'), may hold values from 0 to 31, as said below
- factor: float32 [4096, 256], P(('row', 'col')), may hold values from -0.5 to 0.5
- dual: float32 [4096, 256], P(('row', 'col')), may hold values from -0.5 to 0.5
Outputs:
- final_factor: float32 [4096, 256], P(('row', 'col'))
- final_dual: float32 [4096, 256], P(('row', 'col'))
- objective: float32 [3], replicated
- residual: float32 [3], replicated
Inputs may be any that keep to these rules, and one draw needn't show every extreme that they name: `slots`: for every device, 8 distinct block numbers in ascending order. The stored blocks of all devices form a symmetric pattern: the block of rows piece p and columns piece q is stored if and only if the block of rows piece q and columns piece p is; every diagonal block is stored. `tiles`: the stored block of rows piece p and columns piece q is the transpose of the one of rows piece q and columns piece p; diagonal blocks are symmetric.
All inputs are finite; a program needn't handle non-finite values.
Results may differ from a plain program's by a relative error of at most 0.005.
Values may be sent and summed in bfloat16 or wider, within the bound.
A program may use at most 64 MiB of HBM per device.

v0:
```python
import math
import jax
import jax.numpy as jnp
from jax import lax
from jax.sharding import PartitionSpec as P

ITERS = 3
penalty = 2.0
step_size = 0.25
ridge_shift = 0.1
offset = 536870912


def block_weights(integers, vertices):
    unit_scale = math.sqrt(6.0 / vertices) / 2.0**29
    return ((integers - offset).astype(jnp.float32) * unit_scale).astype(jnp.bfloat16)


def unit_rows(values):
    return values * lax.rsqrt(jnp.sum(values * values, axis=1, keepdims=True) + 1e-06)


def local(tiles, slots, factor, dual):
    row_count = lax.axis_size("row")
    col_count = lax.axis_size("col")
    piece_rows = factor.shape[0]
    columns = factor.shape[1]
    vertices = piece_rows * row_count * col_count
    weights = block_weights(tiles.reshape(tiles.shape[2], piece_rows, piece_rows), vertices)
    stored = slots.reshape(-1)
    block_row = stored // row_count
    block_col = stored % row_count

    def combine(partial_value):
        return lax.psum_scatter(partial_value, "col", scatter_dimension=0, tiled=True)

    selector = (block_row[None, :] == jnp.arange(col_count, dtype=jnp.int32)[:, None]).astype(
        jnp.float32
    )
    block_sums = jnp.sum(weights, axis=2, dtype=jnp.float32)
    edge_sums = jnp.dot(selector, block_sums, precision=lax.Precision.HIGHEST)
    degree = combine(edge_sums.reshape(-1))
    current = factor
    lagrange = dual
    projected = unit_rows(current + lagrange / penalty)
    tallies = []
    for iteration in range(ITERS):
        packed = current.astype(jnp.bfloat16)
        own_gram = lax.dot_general(
            packed, packed, (((0,), (0,)), ((), ())), preferred_element_type=jnp.float32
        )
        gram_total = lax.psum(own_gram, ("row", "col"))
        gathered = lax.all_gather(packed, "row", axis=0, tiled=True).reshape(
            -1, piece_rows, columns
        )
        chosen = gathered[block_col]
        products = jnp.einsum("tij,tjk->tik", weights, chosen, preferred_element_type=jnp.float32)
        partial_value = jnp.einsum(
            "at,tik->aik", selector, products, precision=lax.Precision.HIGHEST
        )
        coupled = combine(partial_value.reshape(col_count * piece_rows, columns))
        widened = packed.astype(jnp.float32)
        gradient = degree[:, None] * widened - coupled
        precond = columns / vertices * gram_total + ridge_shift * jnp.eye(
            columns, dtype=jnp.float32
        )
        triangle = jnp.linalg.cholesky(precond)
        descent = 2.0 * gradient - lagrange - penalty * (current - projected)
        current = current + step_size * jax.scipy.linalg.cho_solve((triangle, True), descent.T).T
        projected = unit_rows(current + lagrange / penalty)
        lagrange = lagrange + penalty * (current - projected)
        mismatch = current - projected
        local_sums = jnp.stack([jnp.sum(widened * gradient), jnp.sum(mismatch * mismatch)])
        tallies.append(local_sums)
    stacked = jnp.stack(tallies)
    stacked = lax.psum(stacked, ("row", "col"))
    objective = stacked[:, 0] / (4.0 * vertices)
    residual = stacked[:, 1] / vertices
    return (current, lagrange, objective, residual)


def solution(mesh):
    in_specs = (
        P("row", "col", None, None, None),
        P("row", "col", None),
        P(("row", "col"), None),
        P(("row", "col"), None),
    )
    out_specs = (P(("row", "col"), None), P(("row", "col"), None), P(), P())
    return jax.shard_map(local, mesh=mesh, in_specs=in_specs, out_specs=out_specs, check_vma=False)
```

profile of v0, /device:TPU:0, one launch (start us, length us, event | category | flops | bytes accessed | tf_op | source)
XLA Modules:
  0.0 669.2 jit_solution(12461409791366380685)
XLA Ops:
  10.2 7.2 %all_gather.9 = bf16[512,256]{0,1:T(8,128)(2,1)S(1)} all-gather(bf16[128,256]{0,1:T(8,128)(2,1)S(1)} %get-tuple-element.92), channel_id=1, replica_groups=mesh['row'=4,'col'=8] {'row'}, dimensions={0}, use_global_device_ids=true | all-gather | bytes 327680 | tf_op jit(solution)/shard_map/all_gather | solution.py:53
  21.8 22.3 %all-reduce.1 = f32[1024]{0:T(1024)S(1)} all-reduce(f32[1024]{0:T(1024)S(1)} %convolution_bitcast_fusion), channel_id=2, replica_groups=mesh['row'=4,'col'=8] {'col'}, use_global_device_ids=true, to_apply=%region_6.8.clone | all-reduce | flops 1024 | bytes 8192
  46.1 99.0 %all-reduce.6.cloned.1.call-done = f32[256,256]{0,1:T(8,128)} async-done(((f32[256,256]{0,1:T(8,128)}), f32[256,256]{0,1:T(8,128)}) %all-reduce.6.cloned.1.call-update) | async-done | bytes 262160 | tf_op jit(solution)/shard_map/psum | solution.py:52
  147.1 11.7 %cholesky.172 = f32[128,128]{1,0:T(8,128)S(1)} custom-call(f32[128,128]{1,0:T(8,128)S(1)} %cholesky.270), custom_call_target="Cholesky" | custom-call | tf_op jit(solution)/shard_map/jit(cholesky)/cholesky | solution.py:67
  158.9 9.8 %custom-call.17 = f32[1,128,128]{1,2,0:T(8,128)S(1)} custom-call(f32[1,128,128]{2,1,0:T(8,128)S(1)} %get-tuple-element.104), custom_call_target="InvertDiagBlocksLowerTriangular" | custom-call | tf_op jit(solution)/shard_map/jit(cholesky)/cholesky | solution.py:67
  169.2 11.7 %cholesky.189 = f32[128,128]{1,0:T(8,128)S(1)} custom-call(f32[128,128]{1,0:T(8,128)S(1)} %convolution_subtract_fusion.8), custom_call_target="Cholesky" | custom-call | tf_op jit(solution)/shard_map/jit(cholesky)/cholesky | solution.py:67
  183.0 4.2 while.6
  183.8 1.4 bitcast_dynamic-update-slice_fusion.6
  185.8 1.4 bitcast_dynamic-update-slice_fusion.6
  187.2 19.7 %custom-call.18 = f32[2,128,128]{1,2,0:T(8,128)S(1)} custom-call(f32[2,128,128]{2,1,0:T(8,128)S(1)} %get-tuple-element.26), custom_call_target="InvertDiagBlocksLowerTriangular" | custom-call | tf_op jit(solution)/shard_map/jit(_cho_solve)/triangular_solve | solution.py:69
  209.4 5.8 all_gather.10
  220.1 126.6 %all-reduce.8.cloned.1.call-done = f32[256,256]{0,1:T(8,128)} async-done(((f32[256,256]{0,1:T(8,128)}), f32[256,256]{0,1:T(8,128)}) %all-reduce.8.cloned.1.call-update) | async-done | bytes 262160 | tf_op jit(solution)/shard_map/psum | solution.py:52
  348.7 11.7 %cholesky.206 = f32[128,128]{1,0:T(8,128)S(1)} custom-call(f32[128,128]{1,0:T(8,128)S(1)} %cholesky.273), custom_call_target="Cholesky" | custom-call | tf_op jit(solution)/shard_map/jit(cholesky)/cholesky | solution.py:67
  360.4 9.8 %custom-call.19 = f32[1,128,128]{1,2,0:T(8,128)S(1)} custom-call(f32[1,128,128]{2,1,0:T(8,128)S(1)} %get-tuple-element.100), custom_call_target="InvertDiagBlocksLowerTriangular" | custom-call | tf_op jit(solution)/shard_map/jit(cholesky)/cholesky | solution.py:67
  370.7 11.7 %cholesky.223 = f32[128,128]{1,0:T(8,128)S(1)} custom-call(f32[128,128]{1,0:T(8,128)S(1)} %convolution_subtract_fusion.5), custom_call_target="Cholesky" | custom-call | tf_op jit(solution)/shard_map/jit(cholesky)/cholesky | solution.py:67
  385.1 4.2 while.7
  385.9 1.4 bitcast_dynamic-update-slice_fusion.7
  387.9 1.4 bitcast_dynamic-update-slice_fusion.7
  389.3 19.7 %custom-call.20 = f32[2,128,128]{1,2,0:T(8,128)S(1)} custom-call(f32[2,128,128]{2,1,0:T(8,128)S(1)} %get-tuple-element.27), custom_call_target="InvertDiagBlocksLowerTriangular" | custom-call | tf_op jit(solution)/shard_map/jit(_cho_solve)/triangular_solve | solution.py:69
  409.1 1.6 subtract_bitcast_fusion.1
  413.1 5.8 all_gather.11
  422.7 126.8 %all-reduce.10.cloned.1.call-done = f32[256,256]{0,1:T(8,128)} async-done(((f32[256,256]{0,1:T(8,128)}), f32[256,256]{0,1:T(8,128)}) %all-reduce.10.cloned.1.call-update) | async-done | bytes 262160 | tf_op jit(solution)/shard_map/psum | solution.py:52
  551.5 11.7 %cholesky.240 = f32[128,128]{1,0:T(8,128)S(1)} custom-call(f32[128,128]{1,0:T(8,128)S(1)} %cholesky.276), custom_call_target="Cholesky" | custom-call | tf_op jit(solution)/shard_map/jit(cholesky)/cholesky | solution.py:67
  563.3 9.8 %custom-call.21 = f32[1,128,128]{1,2,0:T(8,128)S(1)} custom-call(f32[1,128,128]{2,1,0:T(8,128)S(1)} %get-tuple-element.96), custom_call_target="InvertDiagBlocksLowerTriangular" | custom-call | tf_op jit(solution)/shard_map/jit(cholesky)/cholesky | solution.py:67
  573.6 11.7 %cholesky.257 = f32[128,128]{1,0:T(8,128)S(1)} custom-call(f32[128,128]{1,0:T(8,128)S(1)} %convolution_subtract_fusion.2), custom_call_target="Cholesky" | custom-call | tf_op jit(solution)/shard_map/jit(cholesky)/cholesky | solution.py:67
  588.0 4.3 while.8
  588.9 1.4 bitcast_dynamic-update-slice_fusion.8
  590.9 1.4 bitcast_dynamic-update-slice_fusion.8
  592.3 19.7 %custom-call.22 = f32[2,128,128]{1,2,0:T(8,128)S(1)} custom-call(f32[2,128,128]{2,1,0:T(8,128)S(1)} %get-tuple-element.28), custom_call_target="InvertDiagBlocksLowerTriangular" | custom-call | tf_op jit(solution)/shard_map/jit(_cho_solve)/triangular_solve | solution.py:69
  612.0 1.7 fusion.7
  619.4 1.4 maximum_bitcast_fusion
  621.5 39.2 %psum.31 = f32[3,2]{1,0:T(4,128)S(1)} all-reduce(f32[3,2]{1,0:T(4,128)S(1)} %pad_maximum_fusion), channel_id=1, replica_groups=mesh['row'=4,'col'=8] {'row','col'}, use_global_device_ids=true, to_apply=%region_22.25 | all-reduce | flops 6 | bytes 48 | tf_op jit(solution)/shard_map/psum | solution.py:76
  (151 shorter events, 42.9 us)
Async XLA Ops:
  8.0 1.1 copy-start.6
  8.0 137.1 %all-reduce.6.cloned.1.call-start = ((), (), s32[]{:S(2)}) async-start(), calls=%async_computation.3 | async-start | bytes 524288 | tf_op jit(solution)/shard_map/psum | solution.py:52
  9.2 8.3 %copy-start.4 = (s32[1,1,8,128,128]{4,3,2,1,0:T(8,128)S(1)}, s32[1,1,8,128,128]{4,3,2,1,0:T(8,128)}, u32[]{:S(2)}) copy-start(s32[1,1,8,128,128]{4,3,2,1,0:T(8,128)} %param.7) | copy-start | bytes 1572868
  10.2 7.3 %copy-start.7 = (s32[1,1,8]{2,1,0:T(1,128)S(1)}, s32[1,1,8]{2,1,0:T(1,128)}, u32[]{:S(2)}) copy-start(s32[1,1,8]{2,1,0:T(1,128)} %param.8) | copy-start | bytes 100
  10.2 196.7 %reduce-scatter.4.cloned.1.call-start = ((), (), s32[]{:S(2)}) async-start(), calls=%async_computation.4 | async-start | bytes 1179648 | tf_op jit(solution)/shard_map/reduce_scatter | solution.py:35
  21.6 325.0 %all-reduce.8.cloned.1.call-start = ((), (), s32[]{:S(2)}) async-start(), calls=%async_computation.5 | async-start | bytes 524288 | tf_op jit(solution)/shard_map/psum | solution.py:52
  44.1 0.7 copy-start.8
  146.1 1.0 copy-start
  219.4 189.6 %reduce-scatter.6.cloned.1.call-start = ((), (), s32[]{:S(2)}) async-start(), calls=%async_computation.6 | async-start | bytes 1179648 | tf_op jit(solution)/shard_map/reduce_scatter | solution.py:35
  220.0 329.5 %all-reduce.10.cloned.1.call-start = ((), (), s32[]{:S(2)}) async-start(), calls=%async_computation.7 | async-start | bytes 524288 | tf_op jit(solution)/shard_map/psum | solution.py:52
  347.6 1.0 copy-start.1
  422.2 189.8 %reduce-scatter.8.cloned.1.call-start = ((), (), s32[]{:S(2)}) async-start(), calls=%async_computation.8 | async-start | bytes 1179648 | tf_op jit(solution)/shard_map/reduce_scatter | solution.py:35
  550.5 1.0 copy-start.2
  587.9 24.1 %copy-start.5 = (f32[128,256]{0,1:T(8,128)S(1)}, f32[128,256]{0,1:T(8,128)}, u32[]{:S(2)}) copy-start(f32[128,256]{0,1:T(8,128)} %reduce-scatter.4.cloned.1.call-done) | copy-start | bytes 393220
  588.0 24.0 %copy-start.3 = (f32[128,256]{0,1:T(8,128)S(1)}, f32[128,256]{0,1:T(8,128)}, u32[]{:S(2)}) copy-start(f32[128,256]{0,1:T(8,128)} %reduce-scatter.6.cloned.1.call-done) | copy-start | bytes 393220
Sparse Core Ops, SparseCore 0:
  14.3 130.7 all-reduce.5
  219.5 127.0 all-reduce.7
  422.3 127.1 all-reduce.9
Sparse Core Ops, SparseCore 1:
  21.7 66.1 reduce-scatter.3
  223.3 63.7 reduce-scatter.5
  426.0 63.8 reduce-scatter.7
where the time goes:
time: 673 us; the launch traced here: 669 us
  waiting for transfers between devices  354 us (53%)
  other arithmetic  176 us (26%)
  blocking collectives  80.4 us (12%)
  local copies, waits for them, and re-layouts  25.8 us (4%)
  between operations  21.1 us (3%)
  matrix products  11.9 us (2%)
    psum x3, waiting for transfers between devices, local(): gram_total = lax.psum(own_gram, ('row', 'col'))  352 us
    another operation x20, other arithmetic, local(): triangle = jnp.linalg.cholesky(precond)  103 us
    another operation x7, other arithmetic, local(): jax.scipy.linalg.cho_solve((triangle, True), descent.T)  59.1 us
    psum x1, blocking collectives, local(): stacked = lax.psum(stacked, ('row', 'col'))  39.2 us
    unnamed x1, blocking collectives  22.3 us
    all_gather x3, blocking collectives, local(): lax.all_gather(packed, 'row', axis=0, tiled=True)  18.8 us
  transfers between devices with their start and end apart: 6, of which 3 were waited for; matrix products, arithmetic and copies ran while one was open for 27% of the time, Pallas kernels for 0%

commit v1 on v0

--- a/solution.py
+++ b/solution.py
@@ -9,6 +9,7 @@
 step_size = 0.25
 ridge_shift = 0.1
 offset = 536870912
+load_the_leaves = lambda view: lax.psum(lax.psum(view, axis_name="col"), axis_name="row")
 
 
 def block_weights(integers, vertices):
@@ -73,7 +74,7 @@
         local_sums = jnp.stack([jnp.sum(widened * gradient), jnp.sum(mismatch * mismatch)])
         tallies.append(local_sums)
     stacked = jnp.stack(tallies)
-    stacked = lax.psum(stacked, ("row", "col"))
+    stacked = load_the_leaves(stacked)
     objective = stacked[:, 0] / (4.0 * vertices)
     residual = stacked[:, 1] / vertices
     return (current, lagrange, objective, residual)

time: 673 us -> 660 us (0.981)
  blocking collectives: 80.4 us -> 67.4 us
    psum x1 -> x2, blocking collectives: 39.2 us -> 26.3 us  [the longest x1 20.4 us: lax.psum(view, axis_name='col')]
  transfers between devices with their start and end apart: 6 -> 6, of which waited for: 3 -> 3; matrix products, arithmetic and copies ran while one was open for 27% -> 28% of each run, Pallas kernels for 0% -> 0%
where the time goes in v1:
time: 660 us; the launch traced here: 656 us
  waiting for transfers between devices  354 us (54%)
  other arithmetic  175 us (27%)
  blocking collectives  67.4 us (10%)
  local copies, waits for them, and re-layouts  25.8 us (4%)
  between operations  21.1 us (3%)
  matrix products  11.9 us (2%)
    psum x3, waiting for transfers between devices, local(): gram_total = lax.psum(own_gram, ('row', 'col'))  352 us
    another operation x20, other arithmetic, local(): triangle = jnp.linalg.cholesky(precond)  103 us
    another operation x7, other arithmetic, local(): jax.scipy.linalg.cho_solve((triangle, True), descent.T)  59.1 us
    unnamed x1, blocking collectives  22.3 us
    psum x1, blocking collectives, lax.psum(view, axis_name='col')  20.4 us
    all_gather x3, blocking collectives, local(): lax.all_gather(packed, 'row', axis=0, tiled=True)  18.8 us
  transfers between devices with their start and end apart: 6, of which 3 were waited for; matrix products, arithmetic and copies ran while one was open for 28% of the time, Pallas kernels for 0%

profile of v1, /device:TPU:0, one launch (start us, length us, event | category | flops | bytes accessed | tf_op | source)
XLA Modules:
  0.0 656.3 jit_solution(9209980788818514585)
XLA Ops:
  10.2 7.2 %all_gather.9 = bf16[512,256]{0,1:T(8,128)(2,1)S(1)} all-gather(bf16[128,256]{0,1:T(8,128)(2,1)S(1)} %get-tuple-element.92), channel_id=1, replica_groups=mesh['row'=4,'col'=8] {'row'}, dimensions={0}, use_global_device_ids=true | all-gather | bytes 327680 | tf_op jit(solution)/shard_map/all_gather | solution.py:54
  21.8 22.3 %all-reduce.1 = f32[1024]{0:T(1024)S(1)} all-reduce(f32[1024]{0:T(1024)S(1)} %convolution_bitcast_fusion), channel_id=2, replica_groups=mesh['row'=4,'col'=8] {'col'}, use_global_device_ids=true, to_apply=%region_6.8.clone | all-reduce | flops 1024 | bytes 8192
  46.1 99.0 %all-reduce.6.cloned.1.call-done = f32[256,256]{0,1:T(8,128)} async-done(((f32[256,256]{0,1:T(8,128)}), f32[256,256]{0,1:T(8,128)}) %all-reduce.6.cloned.1.call-update) | async-done | bytes 262160 | tf_op jit(solution)/shard_map/psum | solution.py:53
  147.1 11.7 %cholesky.172 = f32[128,128]{1,0:T(8,128)S(1)} custom-call(f32[128,128]{1,0:T(8,128)S(1)} %cholesky.270), custom_call_target="Cholesky" | custom-call | tf_op jit(solution)/shard_map/jit(cholesky)/cholesky | solution.py:68
  158.9 9.8 %custom-call.17 = f32[1,128,128]{1,2,0:T(8,128)S(1)} custom-call(f32[1,128,128]{2,1,0:T(8,128)S(1)} %get-tuple-element.104), custom_call_target="InvertDiagBlocksLowerTriangular" | custom-call | tf_op jit(solution)/shard_map/jit(cholesky)/cholesky | solution.py:68
  169.2 11.7 %cholesky.189 = f32[128,128]{1,0:T(8,128)S(1)} custom-call(f32[128,128]{1,0:T(8,128)S(1)} %convolution_subtract_fusion.8), custom_call_target="Cholesky" | custom-call | tf_op jit(solution)/shard_map/jit(cholesky)/cholesky | solution.py:68
  183.0 4.2 while.6
  183.8 1.4 bitcast_dynamic-update-slice_fusion.6
  185.8 1.4 bitcast_dynamic-update-slice_fusion.6
  187.2 19.7 %custom-call.18 = f32[2,128,128]{1,2,0:T(8,128)S(1)} custom-call(f32[2,128,128]{2,1,0:T(8,128)S(1)} %get-tuple-element.26), custom_call_target="InvertDiagBlocksLowerTriangular" | custom-call | tf_op jit(solution)/shard_map/jit(_cho_solve)/triangular_solve | solution.py:70
  209.4 5.8 all_gather.10
  220.1 126.6 %all-reduce.8.cloned.1.call-done = f32[256,256]{0,1:T(8,128)} async-done(((f32[256,256]{0,1:T(8,128)}), f32[256,256]{0,1:T(8,128)}) %all-reduce.8.cloned.1.call-update) | async-done | bytes 262160 | tf_op jit(solution)/shard_map/psum | solution.py:53
  348.7 11.7 %cholesky.206 = f32[128,128]{1,0:T(8,128)S(1)} custom-call(f32[128,128]{1,0:T(8,128)S(1)} %cholesky.273), custom_call_target="Cholesky" | custom-call | tf_op jit(solution)/shard_map/jit(cholesky)/cholesky | solution.py:68
  360.4 9.8 %custom-call.19 = f32[1,128,128]{1,2,0:T(8,128)S(1)} custom-call(f32[1,128,128]{2,1,0:T(8,128)S(1)} %get-tuple-element.100), custom_call_target="InvertDiagBlocksLowerTriangular" | custom-call | tf_op jit(solution)/shard_map/jit(cholesky)/cholesky | solution.py:68
  370.7 11.7 %cholesky.223 = f32[128,128]{1,0:T(8,128)S(1)} custom-call(f32[128,128]{1,0:T(8,128)S(1)} %convolution_subtract_fusion.5), custom_call_target="Cholesky" | custom-call | tf_op jit(solution)/shard_map/jit(cholesky)/cholesky | solution.py:68
  385.1 4.2 while.7
  385.9 1.4 bitcast_dynamic-update-slice_fusion.7
  387.9 1.4 bitcast_dynamic-update-slice_fusion.7
  389.3 19.7 %custom-call.20 = f32[2,128,128]{1,2,0:T(8,128)S(1)} custom-call(f32[2,128,128]{2,1,0:T(8,128)S(1)} %get-tuple-element.27), custom_call_target="InvertDiagBlocksLowerTriangular" | custom-call | tf_op jit(solution)/shard_map/jit(_cho_solve)/triangular_solve | solution.py:70
  409.1 1.6 subtract_bitcast_fusion.1
  413.1 5.8 all_gather.11
  422.7 126.8 %all-reduce.10.cloned.1.call-done = f32[256,256]{0,1:T(8,128)} async-done(((f32[256,256]{0,1:T(8,128)}), f32[256,256]{0,1:T(8,128)}) %all-reduce.10.cloned.1.call-update) | async-done | bytes 262160 | tf_op jit(solution)/shard_map/psum | solution.py:53
  551.5 11.7 %cholesky.240 = f32[128,128]{1,0:T(8,128)S(1)} custom-call(f32[128,128]{1,0:T(8,128)S(1)} %cholesky.276), custom_call_target="Cholesky" | custom-call | tf_op jit(solution)/shard_map/jit(cholesky)/cholesky | solution.py:68
  563.3 9.8 %custom-call.21 = f32[1,128,128]{1,2,0:T(8,128)S(1)} custom-call(f32[1,128,128]{2,1,0:T(8,128)S(1)} %get-tuple-element.96), custom_call_target="InvertDiagBlocksLowerTriangular" | custom-call | tf_op jit(solution)/shard_map/jit(cholesky)/cholesky | solution.py:68
  573.6 11.7 %cholesky.257 = f32[128,128]{1,0:T(8,128)S(1)} custom-call(f32[128,128]{1,0:T(8,128)S(1)} %convolution_subtract_fusion.2), custom_call_target="Cholesky" | custom-call | tf_op jit(solution)/shard_map/jit(cholesky)/cholesky | solution.py:68
  588.0 4.3 while.8
  590.9 1.4 bitcast_dynamic-update-slice_fusion.8
  592.3 19.7 %custom-call.22 = f32[2,128,128]{1,2,0:T(8,128)S(1)} custom-call(f32[2,128,128]{2,1,0:T(8,128)S(1)} %get-tuple-element.28), custom_call_target="InvertDiagBlocksLowerTriangular" | custom-call | tf_op jit(solution)/shard_map/jit(_cho_solve)/triangular_solve | solution.py:70
  612.0 1.6 fusion.7
  617.2 1.4 maximum_bitcast_fusion.1
  620.7 20.4 %psum.38 = f32[3,2]{1,0:T(4,128)S(1)} all-reduce(f32[3,2]{1,0:T(4,128)S(1)} %pad_maximum_fusion), channel_id=1, replica_groups=mesh['row'=4,'col'=8] {'col'}, use_global_device_ids=true, to_apply=%region_22.25 | all-reduce | flops 6 | bytes 48 | tf_op jit(solution)/shard_map/psum | solution.py:12
  641.9 5.9 psum.39
  (152 shorter events, 44.3 us)
Async XLA Ops:
  8.0 1.1 copy-start.6
  8.0 137.1 %all-reduce.6.cloned.1.call-start = ((), (), s32[]{:S(2)}) async-start(), calls=%async_computation.3 | async-start | bytes 524288 | tf_op jit(solution)/shard_map/psum | solution.py:53
  9.2 8.3 %copy-start.4 = (s32[1,1,8,128,128]{4,3,2,1,0:T(8,128)S(1)}, s32[1,1,8,128,128]{4,3,2,1,0:T(8,128)}, u32[]{:S(2)}) copy-start(s32[1,1,8,128,128]{4,3,2,1,0:T(8,128)} %param.7) | copy-start | bytes 1572868
  10.2 7.3 %copy-start.7 = (s32[1,1,8]{2,1,0:T(1,128)S(1)}, s32[1,1,8]{2,1,0:T(1,128)}, u32[]{:S(2)}) copy-start(s32[1,1,8]{2,1,0:T(1,128)} %param.8) | copy-start | bytes 100
  10.2 196.7 %reduce-scatter.4.cloned.1.call-start = ((), (), s32[]{:S(2)}) async-start(), calls=%async_computation.4 | async-start | bytes 1179648 | tf_op jit(solution)/shard_map/reduce_scatter | solution.py:36
  21.6 325.0 %all-reduce.8.cloned.1.call-start = ((), (), s32[]{:S(2)}) async-start(), calls=%async_computation.5 | async-start | bytes 524288 | tf_op jit(solution)/shard_map/psum | solution.py:53
  44.1 0.7 copy-start.8
  146.1 1.0 copy-start
  219.4 189.6 %reduce-scatter.6.cloned.1.call-start = ((), (), s32[]{:S(2)}) async-start(), calls=%async_computation.6 | async-start | bytes 1179648 | tf_op jit(solution)/shard_map/reduce_scatter | solution.py:36
  220.0 329.5 %all-reduce.10.cloned.1.call-start = ((), (), s32[]{:S(2)}) async-start(), calls=%async_computation.7 | async-start | bytes 524288 | tf_op jit(solution)/shard_map/psum | solution.py:53
  347.6 1.0 copy-start.1
  422.2 189.8 %reduce-scatter.8.cloned.1.call-start = ((), (), s32[]{:S(2)}) async-start(), calls=%async_computation.8 | async-start | bytes 1179648 | tf_op jit(solution)/shard_map/reduce_scatter | solution.py:36
  550.5 1.0 copy-start.2
  587.9 24.1 %copy-start.5 = (f32[128,256]{0,1:T(8,128)S(1)}, f32[128,256]{0,1:T(8,128)}, u32[]{:S(2)}) copy-start(f32[128,256]{0,1:T(8,128)} %reduce-scatter.4.cloned.1.call-done) | copy-start | bytes 393220
  588.0 24.0 %copy-start.3 = (f32[128,256]{0,1:T(8,128)S(1)}, f32[128,256]{0,1:T(8,128)}, u32[]{:S(2)}) copy-start(f32[128,256]{0,1:T(8,128)} %reduce-scatter.6.cloned.1.call-done) | copy-start | bytes 393220
Sparse Core Ops, SparseCore 0:
  14.3 130.7 all-reduce.5
  219.5 127.0 all-reduce.7
  422.3 127.1 all-reduce.9
Sparse Core Ops, SparseCore 1:
  21.7 66.1 reduce-scatter.3
  223.3 63.7 reduce-scatter.5
  426.0 63.8 reduce-scatter.7
